TPU v7x, 128 devices: a whole 4x4x4 slice. The times are simulated.
128 devices in a mesh: dp: 64 (over z, y, x), cp: 2 (over core).
Axes of the slice: x: 4, y: 4, z: 4, core: 2. Of those that a mesh axis runs over, the one named last changes fastest.
Arguments:
- x: bfloat16 [128, 1024, 1024], P('dp', 'cp')
- grad_out: bfloat16 [128, 1024, 1024], P('dp', 'cp')
- w_q: bfloat16 [1024, 16, 64], replicated
- w_k: bfloat16 [1024, 16, 64], replicated
- w_v: bfloat16 [1024, 16, 64], replicated
- w_o: bfloat16 [1024, 16, 64], replicated
- w_up: bfloat16 [1024, 4096], replicated
- w_down: bfloat16 [4096, 1024], replicated
Outputs:
- output 1: bfloat16 [128, 1024, 1024], P('dp', 'cp')
- output 2: float32 [1024, 16, 64], P(('dp', 'cp'))
- output 3: float32 [1024, 16, 64], P(('dp', 'cp'))
- output 4: float32 [1024, 16, 64], P(('dp', 'cp'))
- output 5: float32 [1024, 16, 64], P(('dp', 'cp'))
- output 6: float32 [1024, 4096], P(('dp', 'cp'))
- output 7: float32 [4096, 1024], P(('dp', 'cp'))
All inputs are finite; a program needn't handle non-finite values.
Results may differ from a plain program's by a relative error of at most 0.0130205.
Values are sent between devices in bfloat16 or wider.
A program may use at most 1 GiB of HBM per device.

v0:
```python
import jax
import jax.numpy as jnp
from jax import lax
from jax.sharding import PartitionSpec as P

NEG_BIG = -1e30


def gelu_tanh(values):
    return jax.nn.gelu(values, approximate=True)


def solution(mesh):
    cp_size = mesh.shape['cp']
    dev_count = cp_size * mesh.shape['dp']
    send_perm = [(sender, (sender + 1) % cp_size) for sender in range(cp_size)]

    def reduce_grad(grad):
        return lax.psum_scatter(grad, ('dp', 'cp'), scatter_dimension=0, tiled=True) / dev_count

    def per_device(x_loc, cot_loc, w_q, w_k, w_v, w_o, w_up, w_down):
        batch, seq_len, d_model = x_loc.shape
        kv_heads, head_dim = w_k.shape[1], w_k.shape[2]
        group = w_q.shape[1] // kv_heads
        half = seq_len // 2
        scale = head_dim ** -0.5
        my_idx = lax.axis_index('cp')
        w_q_heads = w_q.reshape(d_model, kv_heads, group, head_dim)
        w_o_heads = w_o.reshape(d_model, kv_heads, group, head_dim)
        offsets = jnp.arange(half)
        local_pos = jnp.concatenate([my_idx * half + offsets, (2 * cp_size - 1 - my_idx) * half + offsets])
        diag_keep = local_pos[None, :] <= local_pos[:, None]

        def fwd_block(q_blk, k_blk, v_blk, state, keep):
            row_max, row_sum, out_sum = state
            scores = jnp.einsum('bkgqe,bkte->bkgqt', q_blk, k_blk, preferred_element_type=jnp.float32) * scale
            if keep is not None:
                scores = jnp.where(keep, scores, NEG_BIG)
            new_max = jnp.maximum(row_max, scores.max(axis=-1))
            alpha = jnp.exp(row_max - new_max)
            exp_scores = jnp.exp(scores - new_max[..., None])
            new_sum = alpha * row_sum + exp_scores.sum(axis=-1)
            new_out = alpha[..., None] * out_sum + jnp.einsum('bkgqt,bkte->bkgqe', exp_scores.astype(jnp.bfloat16), v_blk, preferred_element_type=jnp.float32)
            return new_max, new_sum, new_out

        def bwd_block(q_blk, k_blk, v_blk, grad_o, log_norm, delta, keep):
            scores = jnp.einsum('bkgqe,bkte->bkgqt', q_blk, k_blk, preferred_element_type=jnp.float32) * scale
            if keep is not None:
                scores = jnp.where(keep, scores, NEG_BIG)
            attn_prob = jnp.exp(scores - log_norm[..., None])
            grad_v = jnp.einsum('bkgqt,bkgqe->bkte', attn_prob.astype(jnp.bfloat16), grad_o, preferred_element_type=jnp.float32)
            grad_p = jnp.einsum('bkgqe,bkte->bkgqt', grad_o, v_blk, preferred_element_type=jnp.float32)
            grad_s = (attn_prob * (grad_p - delta[..., None]) * scale).astype(jnp.bfloat16)
            grad_q = jnp.einsum('bkgqt,bkte->bkgqe', grad_s, k_blk, preferred_element_type=jnp.float32)
            grad_k = jnp.einsum('bkgqt,bkgqe->bkte', grad_s, q_blk, preferred_element_type=jnp.float32)
            return grad_q, grad_k, grad_v

        q_heads = jnp.einsum('bsd,dkge->bkgse', x_loc, w_q_heads, preferred_element_type=jnp.float32).astype(jnp.bfloat16)
        k_heads = jnp.einsum('bsd,dke->bkse', x_loc, w_k, preferred_element_type=jnp.float32).astype(jnp.bfloat16)
        v_heads = jnp.einsum('bsd,dke->bkse', x_loc, w_v, preferred_element_type=jnp.float32).astype(jnp.bfloat16)
        kv_own = jnp.stack([k_heads, v_heads])

        stat_shape = (batch, kv_heads, group, seq_len)
        init = (jnp.full(stat_shape, NEG_BIG, jnp.float32), jnp.zeros(stat_shape, jnp.float32),
                jnp.zeros(stat_shape + (head_dim,), jnp.float32))
        state = fwd_block(q_heads, k_heads, v_heads, init, diag_keep)

        def fwd_step(step, carry):
            kv_cur = lax.ppermute(carry[0], 'cp', send_perm)
            src_idx = (my_idx - step) % cp_size

            def lower(args):
                return fwd_block(q_heads, kv_cur[0][:, :, :half], kv_cur[1][:, :, :half], args, None)

            def upper(args):
                part = fwd_block(q_heads[:, :, :, half:], kv_cur[0], kv_cur[1], tuple(piece[:, :, :, half:] for piece in args), None)
                return tuple(lax.dynamic_update_slice_in_dim(full, piece, half, axis=3) for full, piece in zip(args, part))

            return (kv_cur,) + tuple(lax.cond(src_idx < my_idx, lower, upper, carry[1:]))

        _, row_max, row_sum, out_sum = lax.fori_loop(1, cp_size, fwd_step, (kv_own,) + tuple(state))
        o_f32 = out_sum / row_sum[..., None]
        o_heads = o_f32.astype(jnp.bfloat16)
        log_norm = row_max + jnp.log(row_sum)

        h_act = (x_loc + jnp.einsum('bkgse,dkge->bsd', o_heads, w_o_heads, preferred_element_type=jnp.float32)).astype(jnp.bfloat16)
        act_f, gelu_back = jax.vjp(gelu_tanh, jnp.einsum('bsd,df->bsf', h_act, w_up, preferred_element_type=jnp.float32))
        act_out = act_f.astype(jnp.bfloat16)

        grad_w_down = reduce_grad(jnp.einsum('bsf,bsd->fd', act_out, cot_loc, preferred_element_type=jnp.float32))
        grad_act = jnp.einsum('bsd,fd->bsf', cot_loc, w_down, preferred_element_type=jnp.float32).astype(jnp.bfloat16)
        grad_u = gelu_back(grad_act.astype(jnp.float32))[0].astype(jnp.bfloat16)
        grad_w_up = reduce_grad(jnp.einsum('bsd,bsf->df', h_act, grad_u, preferred_element_type=jnp.float32))
        grad_h = cot_loc + jnp.einsum('bsf,df->bsd', grad_u, w_up, preferred_element_type=jnp.float32)
        grad_h_bf = grad_h.astype(jnp.bfloat16)
        grad_w_o = reduce_grad(jnp.einsum('bsd,bkgse->dkge', grad_h_bf, o_heads, preferred_element_type=jnp.float32).reshape(d_model, -1, head_dim))
        grad_o = jnp.einsum('bsd,dkge->bkgse', grad_h_bf, w_o_heads, preferred_element_type=jnp.float32).astype(jnp.bfloat16)
        delta = jnp.sum(grad_o.astype(jnp.float32) * o_f32, axis=-1)

        dq_own, dk_own, dv_own = bwd_block(q_heads, k_heads, v_heads, grad_o, log_norm, delta, diag_keep)

        def bwd_step(step, carry):
            kv_cur = lax.ppermute(carry[0], 'cp', send_perm)
            dkv_cur = lax.ppermute(carry[1], 'cp', send_perm)
            src_idx = (my_idx - step) % cp_size

            def lower(args):
                dkv_acc, grad_q = args
                part_q, part_k, part_v = bwd_block(q_heads, kv_cur[0][:, :, :half], kv_cur[1][:, :, :half], grad_o, log_norm, delta, None)
                new_dkv = lax.dynamic_update_slice_in_dim(dkv_acc, dkv_acc[:, :, :, :half] + jnp.stack([part_k, part_v]), 0, axis=3)
                return new_dkv, grad_q + part_q

            def upper(args):
                dkv_acc, grad_q = args
                part_q, part_k, part_v = bwd_block(q_heads[:, :, :, half:], kv_cur[0], kv_cur[1], grad_o[:, :, :, half:],
                                                   log_norm[:, :, :, half:], delta[:, :, :, half:], None)
                new_q = lax.dynamic_update_slice_in_dim(grad_q, grad_q[:, :, :, half:] + part_q, half, axis=3)
                return dkv_acc + jnp.stack([part_k, part_v]), new_q

            dkv_cur, grad_q = lax.cond(src_idx < my_idx, lower, upper, (dkv_cur, carry[2]))
            return kv_cur, dkv_cur, grad_q

        _, dkv_acc, grad_q = lax.fori_loop(1, cp_size, bwd_step, (kv_own, jnp.stack([dk_own, dv_own]), dq_own))
        dkv_acc = lax.ppermute(dkv_acc, 'cp', send_perm)

        grad_q_bf = grad_q.astype(jnp.bfloat16)
        grad_k_bf = dkv_acc[0].astype(jnp.bfloat16)
        grad_v_bf = dkv_acc[1].astype(jnp.bfloat16)
        grad_w_q = reduce_grad(jnp.einsum('bsd,bkgse->dkge', x_loc, grad_q_bf, preferred_element_type=jnp.float32).reshape(d_model, -1, head_dim))
        grad_w_k = reduce_grad(jnp.einsum('bsd,bkse->dke', x_loc, grad_k_bf, preferred_element_type=jnp.float32))
        grad_w_v = reduce_grad(jnp.einsum('bsd,bkse->dke', x_loc, grad_v_bf, preferred_element_type=jnp.float32))
        grad_x = (grad_h
                  + jnp.einsum('bkgse,dkge->bsd', grad_q_bf, w_q_heads, preferred_element_type=jnp.float32)
                  + jnp.einsum('bkse,dke->bsd', grad_k_bf, w_k, preferred_element_type=jnp.float32)
                  + jnp.einsum('bkse,dke->bsd', grad_v_bf, w_v, preferred_element_type=jnp.float32))
        return grad_x.astype(jnp.bfloat16), grad_w_q, grad_w_k, grad_w_v, grad_w_o, grad_w_up, grad_w_down

    act_spec = P('dp', 'cp', None)
    rep_three = P(None, None, None)
    rep_two = P(None, None)
    grad_three = P(('dp', 'cp'), None, None)
    grad_two = P(('dp', 'cp'), None)
    return jax.shard_map(per_device, mesh=mesh,
                         in_specs=(act_spec, act_spec, rep_three, rep_three, rep_three, rep_three, rep_two, rep_two),
                         out_specs=(act_spec, grad_three, grad_three, grad_three, grad_three, grad_two, grad_two),
                         check_vma=False)
```

profile of v0, /device:TPU:0, one launch (start us, length us, event | category | flops | bytes accessed | tf_op | source)
XLA Modules:
  0.0 4195.0 jit_solution(4862829644903358622)
XLA Ops:
  22.4 13.6 fusion.171
  36.0 13.1 fusion.74
  49.2 16.1 add_bitcast_fusion
  65.3 15.6 conditional.2
  74.4 6.3 fusion.51
  87.6 15.8 fusion.94
  103.4 24.8 fusion.78
  128.2 13.3 fusion.92
  145.4 16.1 fusion.107
  161.5 20.4 multiply_convert_fusion.2
  181.9 9.0 convolution_bitcast_fusion.8
  197.0 19.6 collective-permute-start.1
  221.0 8.1 copy.75
  229.3 11.6 convolution_bitcast_fusion.4
  240.9 39.6 conditional.3
  255.4 9.5 multiply_convert_fusion
  264.9 6.2 fusion.8
  273.4 6.6 maximum_add_fusion
  286.4 8.1 copy.68
  298.8 9.0 collective-permute-start.2
  307.8 6.9 collective-permute-done.2
  321.2 8.1 copy.70
  329.4 6.5 convolution_bitcast_fusion.5
  335.9 8.1 copy.72
  344.1 19.1 convolution_bitcast_fusion.1
  363.5 16.3 convolution_bitcast_fusion.2
  379.8 510.5 %reduce-scatter.13.cloned.1.call-done = f32[8,16,64]{2,1,0:T(8,128)} async-done(((f32[1024,16,64]{2,1,0:T(8,128)}), f32[8,16,64]{2,1,0:T(8,128)}) %reduce-scatter.13.cloned.1.call-update) | async-done | bytes 32784 | tf_op jit(solution)/shard_map/reduce_scatter | solution.py:19
  904.0 639.6 %reduce-scatter.7.cloned.1.call-done = f32[8,16,64]{2,1,0:T(8,128)} async-done(((f32[1024,16,64]{2,1,0:T(8,128)}), f32[8,16,64]{2,1,0:T(8,128)}) %reduce-scatter.7.cloned.1.call-update) | async-done | bytes 32784 | tf_op jit(solution)/shard_map/reduce_scatter | solution.py:19
  1545.1 651.9 %reduce-scatter.9.cloned.1.call-done = f32[8,16,64]{2,1,0:T(8,128)} async-done(((f32[1024,16,64]{2,1,0:T(8,128)}), f32[8,16,64]{2,1,0:T(8,128)}) %reduce-scatter.9.cloned.1.call-update) | async-done | bytes 32784 | tf_op jit(solution)/shard_map/reduce_scatter | solution.py:19
  2198.4 651.7 %reduce-scatter.11.cloned.1.call-done = f32[8,16,64]{2,1,0:T(8,128)} async-done(((f32[1024,16,64]{2,1,0:T(8,128)}), f32[8,16,64]{2,1,0:T(8,128)}) %reduce-scatter.11.cloned.1.call-update) | async-done | bytes 32784 | tf_op jit(solution)/shard_map/reduce_scatter | solution.py:19
  2851.7 666.6 %reduce-scatter.17.cloned.1.call-done = f32[32,1024]{1,0:T(8,128)} async-done(((f32[4096,1024]{1,0:T(8,128)}), f32[32,1024]{1,0:T(8,128)}) %reduce-scatter.17.cloned.1.call-update) | async-done | bytes 131088 | tf_op jit(solution)/shard_map/reduce_scatter | solution.py:19
  3519.9 666.6 %reduce-scatter.15.cloned.1.call-done = f32[8,4096]{1,0:T(8,128)} async-done(((f32[1024,4096]{1,0:T(8,128)}), f32[8,4096]{1,0:T(8,128)}) %reduce-scatter.15.cloned.1.call-update) | async-done | bytes 131088 | tf_op jit(solution)/shard_map/reduce_scatter | solution.py:19
  (117 shorter events, 100.1 us)
Async XLA Ops:
  7.2 73.7 %copy-start = (bf16[1024,16,64]{0,2,1:T(8,128)(2,1)S(1)}, bf16[1024,16,64]{0,2,1:T(8,128)(2,1)}, u32[]{:S(2)}) copy-start(bf16[1024,16,64]{0,2,1:T(8,128)(2,1)} %param.17) | copy-start | bytes 6291460
  7.2 883.1 %reduce-scatter.13.cloned.1.call-start = ((), (), s32[]{:S(2)}) async-start(), calls=%async_computation.9 | async-start | bytes 8454144 | tf_op jit(solution)/shard_map/reduce_scatter | solution.py:19
  7.2 4.8 copy-start.27
  7.2 4.8 copy-start.30
  17.1 48.2 %collective-permute-start = (bf16[2,2,16,512,64]{3,4,1,2,0:T(8,128)(2,1)}, bf16[2,2,16,512,64]{3,4,1,2,0:T(8,128)(2,1)}, u32[]{:S(2)}, u32[]{:S(2)}) collective-permute-start(bf16[2,2,16,512,64]{3,4,1,2,0:T(8,128)(2,1)} %pad_maximum_fusion.1), channel_id=1, source_target_pairs={{0,1},{1,0},{2,3},{3,2},{4,5},{5,4},{6,7},{7,6},{8,9},{9,8},{10,11... | collective-permute-start | bytes 12582920 | tf_op jit(solution)/shard_map/while/body/eval_jaxpr/ppermute | solution.py:69
  17.6 4.8 copy-start.15
  22.4 13.6 copy-start.3
  80.9 80.6 %copy-start.20 = (f32[2,16,1,512]{3,1,0,2:T(8,128)}, f32[2,16,1,512]{3,1,0,2:T(8,128)S(1)}, u32[]{:S(2)}) copy-start(f32[2,16,1,512]{3,1,0,2:T(8,128)S(1)} %get-tuple-element.200) | copy-start | bytes 196612
  128.2 13.3 copy-start.12
  128.2 13.3 copy-start.32
  145.4 16.1 copy-start.23
  161.5 20.4 copy-start.4
  181.9 9.0 copy-start.16
  190.9 25.7 copy-start.13
  190.9 25.7 copy-start.33
  190.9 25.7 copy-start.36
  197.0 43.9 %collective-permute-start.1 = (f32[2,2,16,512,64]{3,4,2,1,0:T(8,128)}, f32[2,2,16,512,64]{3,4,2,1,0:T(8,128)}, u32[]{:S(2)}, u32[]{:S(2)}) collective-permute-start(f32[2,2,16,512,64]{3,4,2,1,0:T(8,128)} %pad_maximum_fusion), channel_id=1, source_target_pairs={{0,1},{1,0},{2,3},{3,2},{4,5},{5,4},{6,7},{7,6},{8,9},{9,8},{10,11... | collective-permute-start | bytes 25165832 | tf_op jit(solution)/shard_map/while/body/eval_jaxpr/ppermute | solution.py:104
  229.2 11.7 copy-start.5
  229.2 11.6 copy-start.21
  229.2 11.6 copy-start.24
  229.2 1314.4 %reduce-scatter.7.cloned.1.call-start = ((), (), s32[]{:S(2)}) async-start(), calls=%async_computation.6 | async-start | bytes 8454144 | tf_op jit(solution)/shard_map/reduce_scatter | solution.py:19
  229.3 11.6 copy-start.10
  244.9 5.8 copy-start.7
  273.4 6.6 copy-start.9
  294.5 1902.4 %reduce-scatter.9.cloned.1.call-start = ((), (), s32[]{:S(2)}) async-start(), calls=%async_computation.7 | async-start | bytes 8454144 | tf_op jit(solution)/shard_map/reduce_scatter | solution.py:19
  294.6 22.2 copy-start.28
  298.8 15.9 collective-permute-start.2
  329.3 2520.8 %reduce-scatter.11.cloned.1.call-start = ((), (), s32[]{:S(2)}) async-start(), calls=%async_computation.8 | async-start | bytes 8454144 | tf_op jit(solution)/shard_map/reduce_scatter | solution.py:19
  344.1 3174.2 %reduce-scatter.17.cloned.1.call-start = ((), (), s32[]{:S(2)}) async-start(), calls=%async_computation.11 | async-start | bytes 16908288 | tf_op jit(solution)/shard_map/reduce_scatter | solution.py:19
  363.3 3823.1 %reduce-scatter.15.cloned.1.call-start = ((), (), s32[]{:S(2)}) async-start(), calls=%async_computation.10 | async-start | bytes 16908288 | tf_op jit(solution)/shard_map/reduce_scatter | solution.py:19
  891.7 4.2 copy-start.29
  899.4 3288.6 %copy-start.1 = (bf16[1024,16,64]{0,2,1:T(8,128)(2,1)S(1)}, bf16[1024,16,64]{0,2,1:T(8,128)(2,1)}, u32[]{:S(2)}) copy-start(bf16[1024,16,64]{0,2,1:T(8,128)(2,1)} %param.17) | copy-start | bytes 6291460
  (10 other events, 27.1 us)
Sparse Core Ops, SparseCore 0:
  229.3 660.9 reduce-scatter.12
  892.6 650.9 reduce-scatter.6
  1546.0 650.9 reduce-scatter.8
  2199.2 650.9 reduce-scatter.10
  2852.4 665.8 reduce-scatter.16
  3520.5 665.8 reduce-scatter.14
where the time goes:
time: 4200 us
  waiting for transfers between devices  3790 us (90%)
  matrix products  266 us (6%)
  other arithmetic  46.3 us (1%)
  local copies, waits for them, and re-layouts  43.5 us (1%)
    reduce_scatter x6, waiting for transfers between devices, reduce_grad(): lax.psum_scatter(grad, ('dp', 'cp'), scatter_dimension=0, tiled=True)  3790 us
  transfers between devices with their start and end apart: 9, of which 7 were waited for; matrix products, arithmetic and copies ran while one was open for 5% of the time, Pallas kernels for 0%

commit v1 on v0

v1 whole, which is shorter than its diff:
```python
import jax
import jax.numpy as jnp
from jax import lax
from jax.sharding import PartitionSpec as P

NEG_BIG = -1e30


def gelu_tanh(values):
    return jax.nn.gelu(values, approximate=True)


def solution(mesh):
    cp_size = mesh.shape['cp']
    dev_count = cp_size * mesh.shape['dp']
    swap = [(0, 1), (1, 0)]
    inv = 1.0 / dev_count

    def per_device(x_loc, cot_loc, w_q, w_k, w_v, w_o, w_up, w_down):
        batch, seq_len, d_model = x_loc.shape
        heads, head_dim = w_k.shape[1], w_k.shape[2]
        inner = heads * head_dim
        ff = w_up.shape[1]
        half = seq_len // 2
        tok = 2 * seq_len
        scale = head_dim ** -0.5
        me = lax.axis_index('cp')

        def gather_row(arr):
            mine = lax.dynamic_index_in_dim(arr, me, 0, keepdims=False)
            other = lax.dynamic_index_in_dim(arr, 1 - me, 0, keepdims=False)
            got = lax.ppermute(other, 'cp', swap)
            first = jnp.where(me == 0, mine, got)
            second = jnp.where(me == 0, got, mine)
            return jnp.concatenate([first[:half], second, first[half:]], axis=0)

        x_row = gather_row(x_loc)
        cot = gather_row(cot_loc)
        wq, wk, wv, wo = (w.reshape(d_model, inner) for w in (w_q, w_k, w_v, w_o))

        def dot(a, b, dims):
            return lax.dot_general(a, b, (dims, ((), ())), preferred_element_type=jnp.float32)

        def heads_of(rows):
            return rows.astype(jnp.bfloat16).reshape(tok, heads, head_dim).transpose(1, 0, 2)

        q = heads_of(dot(x_row, wq, ((1,), (0,))))
        k = heads_of(dot(x_row, wk, ((1,), (0,))))
        v = heads_of(dot(x_row, wv, ((1,), (0,))))

        n_blk = 4
        blk = tok // n_blk
        keep = jnp.arange(blk)[None, :] <= jnp.arange(blk)[:, None]

        def scores_of(i):
            s = jnp.einsum('hqe,hte->hqt', q[:, i * blk:(i + 1) * blk], k[:, :(i + 1) * blk], preferred_element_type=jnp.float32) * scale
            mask = jnp.concatenate([jnp.ones((blk, i * blk), bool), keep], axis=1)
            return jnp.where(mask, s, NEG_BIG)

        o_parts, norms = [], []
        for i in range(n_blk):
            s = scores_of(i)
            m = s.max(axis=-1)
            e = jnp.exp(s - m[..., None])
            l = e.sum(axis=-1)
            o = jnp.einsum('hqt,hte->hqe', e.astype(jnp.bfloat16), v[:, :(i + 1) * blk], preferred_element_type=jnp.float32)
            o_parts.append(o / l[..., None])
            norms.append(m + jnp.log(l))
        o_f32 = jnp.concatenate(o_parts, axis=1)
        o_rows = o_f32.astype(jnp.bfloat16).transpose(1, 0, 2).reshape(tok, inner)

        h_act = (x_row + dot(o_rows, wo, ((1,), (1,)))).astype(jnp.bfloat16)
        act_f, gelu_back = jax.vjp(gelu_tanh, dot(h_act, w_up, ((1,), (0,))))
        act_out = act_f.astype(jnp.bfloat16)

        grad_w_down = dot(act_out, cot, ((0,), (0,)))
        grad_act = dot(cot, w_down, ((1,), (1,))).astype(jnp.bfloat16)
        grad_u = gelu_back(grad_act.astype(jnp.float32))[0].astype(jnp.bfloat16)
        grad_w_up = dot(h_act, grad_u, ((0,), (0,)))
        grad_h = cot.astype(jnp.float32) + dot(grad_u, w_up, ((1,), (1,)))
        grad_h_bf = grad_h.astype(jnp.bfloat16)
        grad_w_o = dot(grad_h_bf, o_rows, ((0,), (0,)))

        def shards(g):
            return (g * inv).reshape(dev_count, -1, d_model)

        def reduce(parts):
            joined = jnp.concatenate(parts, axis=1)
            rows = joined.shape[1]
            return lax.psum_scatter(joined.reshape(dev_count * rows, d_model), ('dp', 'cp'), scatter_dimension=0, tiled=True)

        half_ff = ff // 2
        down_shards = shards(grad_w_down)
        up_lo = shards(grad_w_up[:, :half_ff])
        up_hi = shards(grad_w_up[:, half_ff:])
        out_a = reduce([down_shards, up_lo])
        out_b = reduce([up_hi, shards(grad_w_o)])

        grad_o_rows = dot(grad_h_bf, wo, ((1,), (0,)))
        grad_o = heads_of(grad_o_rows)
        delta = jnp.sum(grad_o.astype(jnp.float32) * o_f32, axis=-1)

        dq_parts = []
        dk = [jnp.zeros((heads, blk, head_dim), jnp.float32)] * n_blk
        dv = [jnp.zeros((heads, blk, head_dim), jnp.float32)] * n_blk
        for i in range(n_blk):
            sl = slice(i * blk, (i + 1) * blk)
            p = jnp.exp(scores_of(i) - norms[i][..., None])
            go = grad_o[:, sl]
            kk, vv = k[:, :(i + 1) * blk], v[:, :(i + 1) * blk]
            dvi = jnp.einsum('hqt,hqe->hte', p.astype(jnp.bfloat16), go, preferred_element_type=jnp.float32)
            dp = jnp.einsum('hqe,hte->hqt', go, vv, preferred_element_type=jnp.float32)
            ds = (p * (dp - delta[:, sl][..., None]) * scale).astype(jnp.bfloat16)
            dq_parts.append(jnp.einsum('hqt,hte->hqe', ds, kk, preferred_element_type=jnp.float32))
            dki = jnp.einsum('hqt,hqe->hte', ds, q[:, sl], preferred_element_type=jnp.float32)
            for j in range(i + 1):
                dk[j] = dk[j] + dki[:, j * blk:(j + 1) * blk]
                dv[j] = dv[j] + dvi[:, j * blk:(j + 1) * blk]

        def rows_of(parts):
            return jnp.concatenate(parts, axis=1).astype(jnp.bfloat16).transpose(1, 0, 2).reshape(tok, inner)

        gq, gk, gv = rows_of(dq_parts), rows_of(dk), rows_of(dv)
        out_c = reduce([shards(dot(x_row, g, ((0,), (0,)))) for g in (gq, gk, gv)])

        grad_x = (grad_h + dot(gq, wq, ((1,), (1,))) + dot(gk, wk, ((1,), (1,))) + dot(gv, wv, ((1,), (1,)))).astype(jnp.bfloat16)
        quarter = half
        first = jnp.concatenate([grad_x[:quarter], grad_x[tok - quarter:]], axis=0)
        second = grad_x[quarter:tok - quarter]
        mine = jnp.where(me == 0, first, second)
        other = jnp.where(me == 0, second, first)
        got = lax.ppermute(other, 'cp', swap)
        gx = jnp.stack([jnp.where(me == 0, mine, got), jnp.where(me == 0, got, mine)])

        rows_down = ff // dev_count
        rows = d_model // dev_count
        n_up = rows * half_ff // d_model
        g_down = out_a[:rows_down]
        g_up = jnp.concatenate([out_a[rows_down:].reshape(rows, half_ff), out_b[:n_up].reshape(rows, half_ff)], axis=1)
        g_o = out_b[n_up:].reshape(rows, heads, head_dim)
        g_q, g_k, g_v = (out_c[i * rows:(i + 1) * rows].reshape(rows, heads, head_dim) for i in range(3))
        return gx, g_q, g_k, g_v, g_o, g_up, g_down

    act_spec = P('dp', 'cp', None)
    rep_three = P(None, None, None)
    rep_two = P(None, None)
    grad_three = P(('dp', 'cp'), None, None)
    grad_two = P(('dp', 'cp'), None)
    return jax.shard_map(per_device, mesh=mesh,
                         in_specs=(act_spec, act_spec, rep_three, rep_three, rep_three, rep_three, rep_two, rep_two),
                         out_specs=(act_spec, grad_three, grad_three, grad_three, grad_three, grad_two, grad_two),
                         check_vma=False)
```

time: 4200 us -> 931 us (0.22)
  waiting for transfers between devices: 3790 us -> 586 us
  matrix products: 266 us -> 212 us
    reduce_scatter x6 -> x3, waiting for transfers between devices: 3790 us -> 583 us  [reduce(): lax.psum_scatter(joined.reshape(dev_count * rows, d_model), ('dp', 'cp'),...]
    dot_general x30 -> x41, matrix products: 266 us -> 212 us  [the longest x17 123 us: dot(): lax.dot_general(a, b, (dims, ((), ())), preferred_element_type=jnp.float32)]
  transfers between devices with their start and end apart: 9 -> 6, of which waited for: 7 -> 4; matrix products, arithmetic and copies ran while one was open for 5% -> 16% of each run, Pallas kernels for 0% -> 0%
where the time goes in v1:
time: 931 us; the launch traced here: 921 us
  waiting for transfers between devices  586 us (63%)
  matrix products  212 us (23%)
  other arithmetic  60.9 us (7%)
  local copies, waits for them, and re-layouts  46.7 us (5%)
  between operations  15.4 us (2%)
    reduce_scatter x3, waiting for transfers between devices, reduce(): lax.psum_scatter(joined.reshape(dev_count * rows, d_model), ('dp', 'cp'),...  583 us
    dot_general x17, matrix products, dot(): lax.dot_general(a, b, (dims, ((), ())), preferred_element_type=jnp.float32)  123 us
    concatenate x3, other arithmetic, reduce(): joined = jnp.concatenate(parts, axis=1)  31.3 us
    dot_general x4, matrix products, per_device(): dp = jnp.einsum('hqe,hte->hqt', go, vv, preferred_element_type=jnp.float32)  26.6 us
    reshape x2, local copies, waits for them, and re-layouts, shards(): return (g * inv).reshape(dev_count, -1, d_model)  19.2 us
    dot_general x4, matrix products, per_device(): jnp.einsum('hqt,hqe->hte', p.astype(jnp.bfloat16), go, preferred_element_...  18.6 us
  transfers between devices with their start and end apart: 6, of which 4 were waited for; matrix products, arithmetic and copies ran while one was open for 16% of the time, Pallas kernels for 0%

profile of v1, /device:TPU:0, one launch (start us, length us, event | category | flops | bytes accessed | tf_op | source)
XLA Modules:
  0.0 921.3 jit_solution(247834211909262517)
XLA Ops:
  32.3 3.3 fusion.109
  41.2 4.5 fusion.112
  52.0 3.6 fusion.10
  58.2 3.8 fusion.103
  67.5 11.6 %fusion.170 = f32[1024,4096]{1,0:T(8,128)} fusion(bf16[1024,1024]{1,0:T(8,128)(2,1)S(1)} %fusion.43, bf16[1024,4096]{1,0:T(8,128)(2,1)S(1)} %bitcast.156), kind=kOutput, calls=%fused_computation.217 | convolution fusion | flops 8589934592 | bytes 27262976 | tf_op jit(solution)/shard_map/dot_general | solution.py:42
  79.1 25.9 %fusion.2 = bf16[1024,4096]{1,0:T(8,128)(2,1)} fusion(f32[1024,4096]{1,0:T(8,128)} %fusion.170, bf16[4096,1024]{1,0:T(8,128)(2,1)} %param.15, bf16[256,1024]{1,0:T(8,128)(2,1)S(1)} %copy-done.56, bf16[512,1024]{1,0:T(8,128)(2,1)} %get-tuple-element.15, bf16[256,1024]{1,0:T(8,128)(2,1)S(1)} %get-tuple-element.21), kind=kOutput, calls=%fused_computation.7 | convolution fusion | flops 8688500736 | bytes 35651584 | tf_op jit(solution)/shard_map/dot_general | solution.py:42
  105.1 13.0 %fusion.171 = f32[1024,1024]{1,0:T(8,128)S(1)} fusion(bf16[1024,4096]{1,0:T(8,128)(2,1)} %fusion.2, bf16[1024,4096]{1,0:T(8,128)(2,1)} %param.14), kind=kOutput, calls=%fused_computation.218 | convolution fusion | flops 8589934592 | bytes 20971520 | tf_op jit(solution)/shard_map/dot_general | solution.py:42
  118.1 4.6 multiply_reduce_fusion
  122.8 6.7 fusion.40
  129.5 5.8 multiply_convert_fusion.4
  136.7 3.4 fusion.136
  140.1 4.9 fusion.30
  145.0 8.3 multiply_convert_fusion.2
  156.1 4.1 fusion.133
  160.2 5.8 fusion.16
  166.0 9.7 %multiply_convert_fusion.1 = bf16[16,256,1024]{2,1,0:T(8,128)(2,1)} fusion(f32[16,256,1024]{2,1,0:T(8,128)S(1)} %bitcast.112, bf16[16,1024,64]{1,2,0:T(8,128)(2,1)} %bitcast.138, f32[16,256]{1,0:T(8,128)S(1)} %get-tuple-element.29, f32[16,256]{1,0:T(8,128)S(1)} %get-tuple-element.42, bf16[16,1024,64]{1,2,0:T(8,128)(2,1)} %bitcast.152), kind=kOutput, calls=%fused_computation.16 | convolution fusion | flops 557842432 | bytes 27820032 | tf_op jit(solution)/shard_map/hqe,hte->hqt/dot_general | solution.py:112
  175.8 6.8 convolution_convert_fusion.4
  206.1 5.3 pad_maximum_fusion.1
  213.0 11.6 %fusion.172 = f32[1024,4096]{1,0:T(8,128)S(1)} fusion(bf16[1024,1024]{1,0:T(8,128)(2,1)S(1)} %copy-done.82, bf16[1024,4096]{1,0:T(8,128)(2,1)} %fusion.2), kind=kOutput, calls=%fused_computation.219 | convolution fusion | flops 8589934592 | bytes 27262976 | tf_op jit(solution)/shard_map/dot_general | solution.py:42
  224.7 6.7 slice_multiply_fusion
  231.4 9.5 %reshape.152 = f32[128,16,1024]{2,1,0:T(8,128)} reshape(f32[1024,2048]{1,0:T(8,128)} %get-tuple-element.8) | data formatting | bytes 16777216 | tf_op jit(solution)/shard_map/reshape | solution.py:85
  240.8 5.2 multiply_bitcast_fusion
  246.1 10.2 %pad_maximum_fusion.2 = f32[128,24,1024]{2,1,0:T(8,128)} fusion(f32[128,8,1024]{2,1,0:T(8,128)S(1)} %multiply_bitcast_fusion, f32[128,16,1024]{2,1,0:T(8,128)} %reshape.152), kind=kLoop, calls=%fused_computation.24 | loop fusion | flops 3145728 | bytes 25165824 | tf_op jit(solution)/shard_map/concatenate | solution.py:88
  256.4 9.7 %reshape.158 = f32[128,16,1024]{2,1,0:T(8,128)} reshape(f32[1024,2048]{1,0:T(8,128)} %get-tuple-element.7) | data formatting | bytes 16777216 | tf_op jit(solution)/shard_map/reshape | solution.py:85
  266.1 18.8 %convolution_multiply_fusion = f32[4096,1024]{1,0:T(8,128)} fusion(f32[1024,4096]{1,0:T(8,128)} %fusion.170, bf16[256,1024]{1,0:T(8,128)(2,1)S(1)} %copy-done.57, bf16[512,1024]{1,0:T(8,128)(2,1)S(1)} %copy-done.40, bf16[256,1024]{1,0:T(8,128)(2,1)S(1)} %copy-done.54), kind=kOutput, calls=%fused_computation.32 | convolution fusion | flops 8638169088 | bytes 35651584 | tf_op jit(solution)/shard_map/dot_general | solution.py:42
  284.9 15.8 %pad_maximum_fusion = f32[128,48,1024]{2,1,0:T(8,128)} fusion(f32[128,16,1024]{2,1,0:T(8,128)S(1)} %copy-done.6, f32[128,32,1024]{2,1,0:T(8,128)} %bitcast.118), kind=kLoop, calls=%fused_computation | loop fusion | flops 6291456 | bytes 50331648 | tf_op jit(solution)/shard_map/concatenate | solution.py:88
  302.3 4.1 fusion.62
  306.5 4.5 fusion.64
  311.1 6.3 fusion.42
  323.0 113.4 %reduce-scatter.4.cloned.1.call-done = f32[24,1024]{1,0:T(8,128)} async-done(((f32[3072,1024]{1,0:T(8,128)}), f32[24,1024]{1,0:T(8,128)}) %reduce-scatter.4.cloned.1.call-update) | async-done | bytes 98320 | tf_op jit(solution)/shard_map/reduce_scatter | solution.py:90
  439.4 221.8 %reduce-scatter.6.cloned.1.call-done = f32[24,1024]{1,0:T(8,128)} async-done(((f32[3072,1024]{1,0:T(8,128)}), f32[24,1024]{1,0:T(8,128)}) %reduce-scatter.6.cloned.1.call-update) | async-done | bytes 98320 | tf_op jit(solution)/shard_map/reduce_scatter | solution.py:90
  663.5 247.7 %reduce-scatter.8.cloned.1.call-done = f32[48,1024]{1,0:T(8,128)} async-done(((f32[6144,1024]{1,0:T(8,128)}), f32[48,1024]{1,0:T(8,128)}) %reduce-scatter.8.cloned.1.call-update) | async-done | bytes 196624 | tf_op jit(solution)/shard_map/reduce_scatter | solution.py:90
  (260 shorter events, 89.5 us)
Async XLA Ops:
  7.2 56.9 %copy-start = (bf16[1024,16,64]{0,2,1:T(8,128)(2,1)S(1)}, bf16[1024,16,64]{0,2,1:T(8,128)(2,1)}, u32[]{:S(2)}) copy-start(bf16[1024,16,64]{0,2,1:T(8,128)(2,1)} %param.13) | copy-start | bytes 6291460
  7.2 429.3 %reduce-scatter.4.cloned.1.call-start = ((), (), s32[]{:S(2)}) async-start(), calls=%async_computation.3 | async-start | bytes 12681216 | tf_op jit(solution)/shard_map/reduce_scatter | solution.py:90
  9.6 3.2 collective-permute-start.1
  11.9 33.8 %collective-permute-start = (bf16[512,1024]{1,0:T(8,128)(2,1)}, bf16[512,1024]{1,0:T(8,128)(2,1)}, u32[]{:S(2)}, u32[]{:S(2)}) collective-permute-start(bf16[512,1024]{1,0:T(8,128)(2,1)} %dynamic-slice_bitcast_fusion.1), channel_id=1, source_target_pairs={{0,1},{1,0},{2,3},{3,2},{4,5},{5,4},{6,7},{7,6},{8,9},{9,8},{10,11... | collective-permute-start | bytes 3145736 | tf_op jit(solution)/shard_map/ppermute | solution.py:32
  12.4 12.7 %copy-start.44 = (pred[256,256]{0,1:T(8,128)(4,1)}, pred[256,256]{0,1:T(8,128)(4,1)S(1)}, u32[]{:S(2)}) copy-start(pred[256,256]{0,1:T(8,128)(4,1)S(1)} %iota_compare_fusion) | copy-start | bytes 196612
  17.4 31.5 %copy-start.12 = (bf16[1024,1024]{0,1:T(8,128)(2,1)}, bf16[1024,1024]{0,1:T(8,128)(2,1)S(1)}, u32[]{:S(2)}) copy-start(bf16[1024,1024]{0,1:T(8,128)(2,1)S(1)} %convolution_convert_fusion.3) | copy-start | bytes 6291460
  19.8 29.1 %copy-start.10 = (bf16[1024,1024]{0,1:T(8,128)(2,1)}, bf16[1024,1024]{0,1:T(8,128)(2,1)S(1)}, u32[]{:S(2)}) copy-start(bf16[1024,1024]{0,1:T(8,128)(2,1)S(1)} %convolution_convert_fusion.2) | copy-start | bytes 6291460
  22.3 18.9 %copy-start.16 = (bf16[1024,1024]{0,1:T(8,128)(2,1)}, bf16[1024,1024]{0,1:T(8,128)(2,1)S(1)}, u32[]{:S(2)}) copy-start(bf16[1024,1024]{0,1:T(8,128)(2,1)S(1)} %convolution_convert_fusion.1) | copy-start | bytes 6291460
  48.9 69.2 %copy-start.53 = (bf16[256,1024]{1,0:T(8,128)(2,1)}, bf16[256,1024]{1,0:T(8,128)(2,1)S(1)}, u32[]{:S(2)}) copy-start(bf16[256,1024]{1,0:T(8,128)(2,1)S(1)} %get-tuple-element.21) | copy-start | bytes 1572868
  67.5 11.6 %copy-start.81 = (bf16[1024,1024]{1,0:T(8,128)(2,1)}, bf16[1024,1024]{1,0:T(8,128)(2,1)S(1)}, u32[]{:S(2)}) copy-start(bf16[1024,1024]{1,0:T(8,128)(2,1)S(1)} %fusion.43) | copy-start | bytes 6291460
  67.5 11.6 %copy-start.56 = (bf16[256,1024]{1,0:T(8,128)(2,1)S(1)}, bf16[256,1024]{1,0:T(8,128)(2,1)}, u32[]{:S(2)}) copy-start(bf16[256,1024]{1,0:T(8,128)(2,1)} %get-tuple-element.22) | copy-start | bytes 1572868
  105.0 13.0 %copy-start.39 = (bf16[512,1024]{1,0:T(8,128)(2,1)S(1)}, bf16[512,1024]{1,0:T(8,128)(2,1)}, u32[]{:S(2)}) copy-start(bf16[512,1024]{1,0:T(8,128)(2,1)} %get-tuple-element.15) | copy-start | bytes 3145732
  105.0 13.1 %copy-start.47 = (f32[16,256,64]{1,2,0:T(8,128)S(1)}, f32[16,256,64]{1,2,0:T(8,128)}, u32[]{:S(2)}) copy-start(f32[16,256,64]{1,2,0:T(8,128)} %fusion.106) | copy-start | bytes 3145732
  105.0 13.1 %copy-start.48 = (f32[16,256,64]{1,2,0:T(8,128)S(1)}, f32[16,256,64]{1,2,0:T(8,128)}, u32[]{:S(2)}) copy-start(f32[16,256,64]{1,2,0:T(8,128)} %fusion.109) | copy-start | bytes 3145732
  105.1 13.1 %copy-start.49 = (f32[16,256,64]{1,2,0:T(8,128)S(1)}, f32[16,256,64]{1,2,0:T(8,128)}, u32[]{:S(2)}) copy-start(f32[16,256,64]{1,2,0:T(8,128)} %fusion.112) | copy-start | bytes 3145732
  122.7 17.4 %copy-start.50 = (bf16[1024,1024]{0,1:T(8,128)(2,1)}, bf16[1024,1024]{0,1:T(8,128)(2,1)S(1)}, u32[]{:S(2)}) copy-start(bf16[1024,1024]{0,1:T(8,128)(2,1)S(1)} %get-tuple-element.41) | copy-start | bytes 6291460
  129.5 10.6 %slice-start.4 = ((s8[12582912]{0:T(1024)(128)(4,1)}), s8[4194304]{0:T(1024)(128)(4,1)S(1)}, s32[]{:S(2)}) async-start(s8[12582912]{0:T(1024)(128)(4,1)} %bitcast.116), calls=%async_computation.10 | async-start | bytes 8388608
  129.5 10.6 %slice-start.5 = ((s8[12582912]{0:T(1024)(128)(4,1)}), s8[4194304]{0:T(1024)(128)(4,1)S(1)}, s32[]{:S(2)}) async-start(s8[12582912]{0:T(1024)(128)(4,1)} %bitcast.116), calls=%async_computation.11 | async-start | bytes 8388608
  136.7 66.7 %copy-start.65 = (bf16[16,256,64]{1,2,0:T(8,128)(2,1)}, bf16[16,256,64]{1,2,0:T(8,128)(2,1)S(1)}, u32[]{:S(2)}) copy-start(bf16[16,256,64]{1,2,0:T(8,128)(2,1)S(1)} %convolution_convert_fusion.5) | copy-start | bytes 1572868
  145.0 15.2 %slice-start = ((s8[16777216]{0:T(1024)(128)(4,1)}), s8[4194304]{0:T(1024)(128)(4,1)S(1)}, s32[]{:S(2)}) async-start(s8[16777216]{0:T(1024)(128)(4,1)} %bitcast.111), calls=%async_computation.6 | async-start | bytes 8388608
  145.0 15.2 %slice-start.1 = ((s8[16777216]{0:T(1024)(128)(4,1)}), s8[4194304]{0:T(1024)(128)(4,1)S(1)}, s32[]{:S(2)}) async-start(s8[16777216]{0:T(1024)(128)(4,1)} %bitcast.111), calls=%async_computation.7 | async-start | bytes 8388608
  145.0 15.2 %slice-start.2 = ((s8[16777216]{0:T(1024)(128)(4,1)}), s8[4194304]{0:T(1024)(128)(4,1)S(1)}, s32[]{:S(2)}) async-start(s8[16777216]{0:T(1024)(128)(4,1)} %bitcast.111), calls=%async_computation.8 | async-start | bytes 8388608
  182.7 20.7 %copy-start.71 = (bf16[16,256,64]{1,2,0:T(8,128)(2,1)}, bf16[16,256,64]{1,2,0:T(8,128)(2,1)S(1)}, u32[]{:S(2)}) copy-start(bf16[16,256,64]{1,2,0:T(8,128)(2,1)S(1)} %convolution_convert_fusion.4) | copy-start | bytes 1572868
  186.6 9.5 %copy-start.32 = (bf16[16,256,64]{1,2,0:T(8,128)(2,1)}, bf16[16,256,64]{1,2,0:T(8,128)(2,1)S(1)}, u32[]{:S(2)}) copy-start(bf16[16,256,64]{1,2,0:T(8,128)(2,1)S(1)} %slice.377) | copy-start | bytes 1572868
  211.4 449.7 %reduce-scatter.6.cloned.1.call-start = ((), (), s32[]{:S(2)}) async-start(), calls=%async_computation.4 | async-start | bytes 12681216 | tf_op jit(solution)/shard_map/reduce_scatter | solution.py:90
  256.3 654.9 %reduce-scatter.8.cloned.1.call-start = ((), (), s32[]{:S(2)}) async-start(), calls=%async_computation.5 | async-start | bytes 25362432 | tf_op jit(solution)/shard_map/reduce_scatter | solution.py:90
  256.4 9.8 %copy-start.40 = (bf16[512,1024]{1,0:T(8,128)(2,1)S(1)}, bf16[512,1024]{1,0:T(8,128)(2,1)}, u32[]{:S(2)}) copy-start(bf16[512,1024]{1,0:T(8,128)(2,1)} %get-tuple-element.15) | copy-start | bytes 3145732
  256.4 9.7 %copy-start.54 = (bf16[256,1024]{1,0:T(8,128)(2,1)S(1)}, bf16[256,1024]{1,0:T(8,128)(2,1)}, u32[]{:S(2)}) copy-start(bf16[256,1024]{1,0:T(8,128)(2,1)} %copy-done.53) | copy-start | bytes 1572868
  256.4 9.7 %copy-start.57 = (bf16[256,1024]{1,0:T(8,128)(2,1)S(1)}, bf16[256,1024]{1,0:T(8,128)(2,1)}, u32[]{:S(2)}) copy-start(bf16[256,1024]{1,0:T(8,128)(2,1)} %get-tuple-element.22) | copy-start | bytes 1572868
  266.1 18.8 %copy-start.6 = (f32[128,16,1024]{2,1,0:T(8,128)S(1)}, f32[128,16,1024]{2,1,0:T(8,128)}, u32[]{:S(2)}) copy-start(f32[128,16,1024]{2,1,0:T(8,128)} %reshape.158) | copy-start | bytes 25165828
  317.8 2.8 collective-permute-start.2
  320.7 593.6 %copy-start.1 = (bf16[1024,16,64]{0,2,1:T(8,128)(2,1)S(1)}, bf16[1024,16,64]{0,2,1:T(8,128)(2,1)}, u32[]{:S(2)}) copy-start(bf16[1024,16,64]{0,2,1:T(8,128)(2,1)} %param.13) | copy-start | bytes 6291460
  (66 other events, 275.1 us)
Sparse Core Ops, SparseCore 0:
  211.6 224.8 reduce-scatter.3
  441.4 219.7 reduce-scatter.5
  666.5 244.6 reduce-scatter.7

commit v2 on v1

v2 whole, which is shorter than its diff:
```python
import functools
import math

import jax
import jax.numpy as jnp
from jax import lax
from jax.experimental import pallas as pl
from jax.experimental.pallas import tpu as pltpu
from jax.sharding import PartitionSpec as P

F32 = jnp.float32
BF16 = jnp.bfloat16
MESH = pl.DeviceIdType.MESH
NEG_BIG = -1e30
BLK = 256
LANES = 128
RING = 4
CHUNKS = 2
VMEM_MAX = 66_000_000
GELU_C = math.sqrt(2.0 / math.pi)
GELU_A = 0.044715
NN = (((1,), (0,)), ((), ()))
NT = (((1,), (1,)), ((), ()))
TN = (((0,), (0,)), ((), ()))


def dot(a, b, dims=NN):
    return lax.dot_general(a, b, dims, preferred_element_type=F32)


def nat_block(core, i):
    return core if i == 0 else 3 - core


def block_rows(index):
    return pl.ds(pl.multiple_of(index * BLK, BLK), BLK)


def meet(devices):
    barrier = pltpu.get_barrier_semaphore()
    for device in devices:
        pl.semaphore_signal(barrier, inc=1, device_id=device, device_id_type=MESH)
    pl.semaphore_wait(barrier, len(devices))


def qkv_kernel(x_hbm, g_hbm, wq_ref, wk_ref, wv_ref, q_ref, k_ref, v_ref, x_out, g_out, loc_sem, send_sem, recv_sem):
    dp, me = lax.axis_index('dp'), lax.axis_index('cp')
    peer = 1 - me
    pairs = ((x_hbm, x_out), (g_hbm, g_out))
    local = []
    for i, (src, dst) in enumerate(pairs):
        for b in range(2):
            local.append(pltpu.make_async_copy(src.at[me, pl.ds(b * BLK, BLK)], dst.at[block_rows(nat_block(me, b))], loc_sem.at[i, b]))
    for copy in local:
        copy.start()
    meet([(dp, peer)])
    remote = []
    for i, (src, dst) in enumerate(pairs):
        for b in range(2):
            remote.append(pltpu.make_async_remote_copy(
                src.at[peer, pl.ds(b * BLK, BLK)], dst.at[block_rows(nat_block(me, b))],
                send_sem.at[i, b], recv_sem.at[i, b], device_id=(dp, peer), device_id_type=MESH))
    for copy in remote:
        copy.start()

    def project(core):
        rows = [block_rows(nat_block(core, b)) for b in range(2)]
        xs = jnp.concatenate([x_out[r, :] for r in rows], axis=0)
        for w_ref, out in ((wq_ref, q_ref), (wk_ref, k_ref), (wv_ref, v_ref)):
            val = dot(xs, w_ref[...], NT).astype(BF16)
            for b in range(2):
                out[rows[b], :] = val[b * BLK:(b + 1) * BLK]

    local[0].wait()
    local[1].wait()
    project(me)
    remote[0].wait()
    remote[1].wait()
    project(peer)
    for copy in local[2:] + remote[2:]:
        copy.wait()


def qkv_call(x_loc, g_loc, wq, wk, wv):
    rows = 2 * x_loc.shape[1]
    d_model = x_loc.shape[2]
    act = jax.ShapeDtypeStruct((rows, d_model), BF16)
    any_spec = pl.BlockSpec(memory_space=pl.ANY)
    vmem = pl.BlockSpec(memory_space=pltpu.VMEM)
    return pl.pallas_call(
        qkv_kernel,
        out_shape=[act] * 5,
        in_specs=[any_spec] * 2 + [vmem] * 3,
        out_specs=[vmem] * 5,
        scratch_shapes=[pltpu.SemaphoreType.DMA((2, 2))] * 3,
        compiler_params=pltpu.CompilerParams(collective_id=0, has_side_effects=True, vmem_limit_bytes=VMEM_MAX),
        name='qkv',
    )(x_loc, g_loc, wq, wk, wv)


def head_rows(head):
    return lax.broadcasted_iota(jnp.int32, (LANES, 1), 0) // 64 == head


def head_lanes(head):
    return lax.broadcasted_iota(jnp.int32, (1, LANES), 1) // 64 == head


def causal_mask():
    return lax.broadcasted_iota(jnp.int32, (BLK, BLK), 0) <= lax.broadcasted_iota(jnp.int32, (BLK, BLK), 1)


def mask_last(vals, fill):
    last = jnp.where(causal_mask(), vals[-BLK:], fill)
    return last if vals.shape[0] == BLK else jnp.concatenate([vals[:-BLK], last], axis=0)


def attn_fwd_kernel(scale, q_ref, k_ref, v_ref, o_ref, ot_ref, lse_ref):
    to_log2 = scale * math.log2(math.e)
    q_t = q_ref[...].T
    v_t = v_ref[...].T
    for n in range(q_ref.shape[0] // BLK):
        rows = slice(n * BLK, (n + 1) * BLK)
        keys = slice(0, (n + 1) * BLK)
        parts = []
        for head in range(2):
            qz = jnp.where(head_rows(head), q_t[:, rows], jnp.zeros((), BF16))
            st = mask_last(dot(k_ref[keys, :], qz), NEG_BIG)
            top = jnp.max(st, axis=0, keepdims=True) * to_log2
            p = jnp.exp2(st * to_log2 - top)
            total = jnp.sum(p, axis=0, keepdims=True)
            ot = dot(v_t[head * 64:(head + 1) * 64, keys], p.astype(BF16))
            parts.append(ot / total)
            lse_ref[0, head:head + 1, rows] = top + jnp.log2(total)
        both = jnp.concatenate(parts, axis=0)
        ot_ref[:, rows] = both
        o_ref[rows, :] = both.T.astype(BF16)


def attn_fwd_call(q, k, v, scale):
    tok, inner = q.shape
    pairs = inner // LANES
    cols = pl.BlockSpec((tok, LANES), lambda i: (0, i))
    return pl.pallas_call(
        functools.partial(attn_fwd_kernel, scale),
        grid=(pairs,),
        out_shape=[jax.ShapeDtypeStruct((tok, inner), BF16), jax.ShapeDtypeStruct((inner, tok), F32),
                   jax.ShapeDtypeStruct((pairs, 2, tok), F32)],
        in_specs=[cols] * 3,
        out_specs=[cols, pl.BlockSpec((LANES, tok), lambda i: (i, 0)), pl.BlockSpec((1, 2, tok), lambda i: (i, 0, 0))],
        compiler_params=pltpu.CompilerParams(vmem_limit_bytes=VMEM_MAX),
        cost_estimate=pl.CostEstimate(flops=4 * tok * tok * inner, bytes_accessed=12 * tok * inner, transcendentals=0),
        name='attn_fwd',
    )(q, k, v)


def attn_bwd_kernel(scale, q_ref, k_ref, v_ref, go_ref, ot_ref, lse_ref, gq_ref, gk_ref, gv_ref, dk_ref, dv_ref):
    to_log2 = scale * math.log2(math.e)
    zero = jnp.zeros((), BF16)
    q_t = q_ref[...].T
    k_t = k_ref[...].T
    go_t = go_ref[...].T
    n_blk = q_ref.shape[0] // BLK
    for n in reversed(range(n_blk)):
        rows = slice(n * BLK, (n + 1) * BLK)
        keys = slice(0, (n + 1) * BLK)
        p_parts, s_parts, go_parts, q_parts, dq_parts = [], [], [], [], []
        for head in range(2):
            feat = slice(head * 64, (head + 1) * 64)
            qz = jnp.where(head_rows(head), q_t[:, rows], zero)
            goz = jnp.where(head_rows(head), go_t[:, rows], zero)
            st = dot(k_ref[keys, :], qz)
            p = mask_last(jnp.exp2(st * to_log2 - lse_ref[0, head:head + 1, rows]), 0.0)
            dp = dot(v_ref[keys, :], goz)
            delta = jnp.sum(go_t[feat, rows].astype(F32) * ot_ref[feat, rows], axis=0, keepdims=True)
            ds = (p * (dp - delta)).astype(BF16)
            dq_parts.append(dot(k_t[feat, keys], ds))
            p_parts.append(p.astype(BF16))
            s_parts.append(ds)
            go_parts.append(jnp.where(head_lanes(head), go_ref[rows, :], zero))
            q_parts.append(jnp.where(head_lanes(head), q_ref[rows, :], zero))
        gq_ref[rows, :] = (jnp.concatenate(dq_parts, axis=0).T * scale).astype(BF16)
        dv = dot(jnp.concatenate(p_parts, axis=1), jnp.concatenate(go_parts, axis=0))
        dk = dot(jnp.concatenate(s_parts, axis=1), jnp.concatenate(q_parts, axis=0))
        if n == n_blk - 1:
            dv_ref[keys, :] = dv
            dk_ref[keys, :] = dk
        else:
            dv_ref[keys, :] += dv
            dk_ref[keys, :] += dk
    gk_ref[...] = (dk_ref[...] * scale).astype(BF16)
    gv_ref[...] = dv_ref[...].astype(BF16)


def attn_bwd_call(q, k, v, go, ot, lse, scale):
    tok, inner = q.shape
    pairs = inner // LANES
    cols = pl.BlockSpec((tok, LANES), lambda i: (0, i))
    return pl.pallas_call(
        functools.partial(attn_bwd_kernel, scale),
        grid=(pairs,),
        out_shape=[jax.ShapeDtypeStruct((tok, inner), BF16)] * 3,
        in_specs=[cols] * 4 + [pl.BlockSpec((LANES, tok), lambda i: (i, 0)), pl.BlockSpec((1, 2, tok), lambda i: (i, 0, 0))],
        out_specs=[cols] * 3,
        scratch_shapes=[pltpu.VMEM((tok, LANES), F32)] * 2,
        compiler_params=pltpu.CompilerParams(vmem_limit_bytes=VMEM_MAX),
        cost_estimate=pl.CostEstimate(flops=10 * tok * tok * inner, bytes_accessed=18 * tok * inner, transcendentals=0),
        name='attn_bwd',
    )(q, k, v, go, ot, lse)


def split_cores(val, n_dp, me):
    parts = val.reshape(n_dp, 2, val.shape[0] // (2 * n_dp), LANES)
    first, second = parts[:, 0], parts[:, 1]
    mine = me == 0
    return jnp.where(mine, first, second), jnp.where(mine, second, first)


def mlp_kernel(inv, n_dp, x_ref, g_ref, o_ref, wo_ref, up_ref, down_ref, dn_keep, dn_send, up_keep, up_send, o_keep, o_send,
               gh_out, go_out, h_ref, gh_ref):
    me = lax.axis_index('cp')
    step = pl.program_id(0)
    d_model = x_ref.shape[1]
    width = up_ref.shape[1]

    @pl.when(step == 0)
    def _():
        h_ref[...] = (x_ref[...].astype(F32) + dot(o_ref[...], wo_ref[...])).astype(BF16)
        gh_ref[...] = g_ref[...].astype(F32)

    u = dot(h_ref[...], up_ref[...])
    ga = dot(g_ref[...], down_ref[...], NT).astype(BF16).astype(F32)
    u2 = u * u
    t = jnp.tanh(u * (GELU_C + (GELU_C * GELU_A) * u2))
    half_t = 0.5 * (1.0 + t)
    act = (u * half_t).astype(BF16)
    slope = half_t + (0.5 * u) * ((1.0 - t) * (1.0 + t)) * (GELU_C + (3.0 * GELU_C * GELU_A) * u2)
    gu = (ga * slope).astype(BF16)

    dn = dot(act, g_ref[...], TN) * inv
    n_here = dn_keep.shape[0]
    for j in range(d_model // LANES):
        keep, send = split_cores(dn[:, j * LANES:(j + 1) * LANES], n_here, me)
        dn_keep[:, :, j] = keep.reshape(n_here, -1, 8, LANES)
        dn_send[:, :, j] = send.reshape(n_here, -1, 8, LANES)

    up = dot(h_ref[...], gu, TN) * inv
    for j in range(width // LANES):
        keep, send = split_cores(up[:, j * LANES:(j + 1) * LANES], n_dp, me)
        up_keep[:, j] = keep
        up_send[:, j] = send

    gh_ref[...] += dot(gu, up_ref[...], NT)

    @pl.when(step == pl.num_programs(0) - 1)
    def _():
        gh_out[...] = gh_ref[...]
        ghb = gh_ref[...].astype(BF16)
        dwo = dot(ghb, o_ref[...], TN) * inv
        for j in range(dwo.shape[1] // LANES):
            keep, send = split_cores(dwo[:, j * LANES:(j + 1) * LANES], n_dp, me)
            o_keep[:, j] = keep
            o_send[:, j] = send
        go_out[...] = dot(ghb, wo_ref[...], NT).astype(BF16)


def mlp_call(x, g, o, wo, w_up, w_down, n_dp, inv):
    tok, d_model = x.shape
    ff = w_up.shape[1]
    width = 512
    steps = ff // width
    whole = pl.BlockSpec((tok, d_model), lambda i: (0, 0), pipeline_mode=pl.Buffered(1))
    down = jax.ShapeDtypeStruct((n_dp, ff // (2 * n_dp * 8), d_model // LANES, 8, LANES), F32)
    up = jax.ShapeDtypeStruct((n_dp, ff // LANES, 8, LANES), F32)
    out = jax.ShapeDtypeStruct((n_dp, d_model // LANES, 8, LANES), F32)
    down_spec = pl.BlockSpec((n_dp // steps,) + down.shape[1:], lambda i: (i, 0, 0, 0, 0))
    up_spec = pl.BlockSpec((n_dp, width // LANES, 8, LANES), lambda i: (0, i, 0, 0))
    out_spec = pl.BlockSpec(out.shape, lambda i: (0, 0, 0, 0), pipeline_mode=pl.Buffered(1))
    return pl.pallas_call(
        functools.partial(mlp_kernel, inv, n_dp),
        grid=(steps,),
        out_shape=[down, down, up, up, out, out, jax.ShapeDtypeStruct((tok, d_model), F32),
                   jax.ShapeDtypeStruct((tok, d_model), BF16)],
        in_specs=[whole] * 4 + [pl.BlockSpec((d_model, width), lambda i: (0, i)), pl.BlockSpec((width, d_model), lambda i: (i, 0))],
        out_specs=[down_spec, down_spec, up_spec, up_spec, out_spec, out_spec, whole, whole],
        scratch_shapes=[pltpu.VMEM((tok, d_model), BF16), pltpu.VMEM((tok, d_model), F32)],
        compiler_params=pltpu.CompilerParams(vmem_limit_bytes=VMEM_MAX),
        cost_estimate=pl.CostEstimate(flops=10 * tok * d_model * ff, bytes_accessed=4 * 2 * d_model * ff, transcendentals=0),
        name='mlp',
    )(x, g, o, wo, w_up, w_down)


def dqkv_kernel(inv, n_dp, x_ref, gq_ref, gk_ref, gv_ref, keep_ref, send_ref):
    me = lax.axis_index('cp')
    for i, ref in enumerate((gq_ref, gk_ref, gv_ref)):
        dw = dot(x_ref[...], ref[...], TN) * inv
        for j in range(dw.shape[1] // LANES):
            keep, send = split_cores(dw[:, j * LANES:(j + 1) * LANES], n_dp, me)
            keep_ref[:, i, j] = keep
            send_ref[:, i, j] = send


def dqkv_call(x, gq, gk, gv, n_dp, inv):
    tok, d_model = x.shape
    inner = gq.shape[1]
    width = 256
    whole = pl.BlockSpec((tok, d_model), lambda i: (0, 0), pipeline_mode=pl.Buffered(1))
    cols = pl.BlockSpec((tok, width), lambda i: (0, i))
    out = jax.ShapeDtypeStruct((n_dp, 3, inner // LANES, 8, LANES), F32)
    spec = pl.BlockSpec((n_dp, 3, width // LANES, 8, LANES), lambda i: (0, 0, i, 0, 0))
    return pl.pallas_call(
        functools.partial(dqkv_kernel, inv, n_dp),
        grid=(inner // width,),
        out_shape=[out, out],
        in_specs=[whole, cols, cols, cols],
        out_specs=[spec, spec],
        compiler_params=pltpu.CompilerParams(vmem_limit_bytes=VMEM_MAX),
        cost_estimate=pl.CostEstimate(flops=6 * tok * d_model * inner, bytes_accessed=12 * d_model * inner, transcendentals=0),
        name='dqkv',
    )(x, gq, gk, gv)


def gx_kernel(gq_ref, gk_ref, gv_ref, wq_ref, wk_ref, wv_ref, gh_ref, out_hbm, stage, loc_sem, send_sem, recv_sem):
    dp, me = lax.axis_index('dp'), lax.axis_index('cp')
    peer = 1 - me
    meet([(dp, peer)])

    def rows_of(core, slot):
        rows = [block_rows(nat_block(core, b)) for b in range(2)]

        def both(ref):
            return jnp.concatenate([ref[r, :] for r in rows], axis=0)

        total = both(gh_ref)
        for ref, w_ref in ((gq_ref, wq_ref), (gk_ref, wk_ref), (gv_ref, wv_ref)):
            total += dot(both(ref), w_ref[...])
        stage[slot] = total.astype(BF16)

    rows_of(peer, 0)
    away = pltpu.make_async_remote_copy(stage.at[0], out_hbm.at[me], send_sem, recv_sem, device_id=(dp, peer), device_id_type=MESH)
    away.start()
    rows_of(me, 1)
    home = pltpu.make_async_copy(stage.at[1], out_hbm.at[me], loc_sem)
    home.start()
    home.wait()
    away.wait()


def gx_call(gq, gk, gv, wq, wk, wv, gh):
    tok, d_model = gh.shape
    vmem = pl.BlockSpec(memory_space=pltpu.VMEM)
    return pl.pallas_call(
        gx_kernel,
        out_shape=jax.ShapeDtypeStruct((2, tok // 2, d_model), BF16),
        in_specs=[vmem] * 7,
        out_specs=pl.BlockSpec(memory_space=pl.ANY),
        scratch_shapes=[pltpu.VMEM((2, tok // 2, d_model), BF16)] + [pltpu.SemaphoreType.DMA] * 3,
        compiler_params=pltpu.CompilerParams(collective_id=1, has_side_effects=True, vmem_limit_bytes=VMEM_MAX),
        name='gx',
    )(gq, gk, gv, wq, wk, wv, gh)


class Color:
    def __init__(self, axes, chunks):
        self.axes = axes
        self.chunks = chunks


def rs_plan():
    down = [[(0, i * 128, 128)] for i in range(2)]
    up = [[(1, i * 128, 128)] for i in range(2)]
    attn = [[(2, 0, 64), (3, 0, 64)], [(3, 64, 128)]]
    return [Color((2, 1, 0), down), Color((1, 0, 2), up), Color((0, 2, 1), attn)]


def rs_kernel(plan, *refs):
    n_in = 1 + max(piece[0] for color in plan for chunk in color.chunks for piece in chunk)
    keep, recv, out_ref = refs[:n_in], refs[n_in:2 * n_in], refs[2 * n_in]
    own, tmp, r1a, r1b, r2a, r2b, r3a, r3b, keep_sem, part_sem, send_sem, recv_sem = refs[2 * n_in + 1:]
    got = ((r1a, r1b), (r2a, r2b), (r3a, r3b))
    rows = own.shape[5]
    half = rows // 2
    dp, cp = lax.axis_index('dp'), lax.axis_index('cp')
    coords = (dp // 16, (dp // 4) % 4, dp % 4)

    def neighbor(axis, delta):
        at = list(coords)
        at[axis] = (coords[axis] + delta) % RING
        return (at[0] * 16 + at[1] * 4 + at[2], cp)

    def group(color, phase, delta):
        index = [slice(None)] * 3
        for axis in color.axes[:phase]:
            index[axis] = coords[axis]
        axis = color.axes[phase]
        index[axis] = (coords[axis] + delta) % RING
        return tuple(index)

    def add_into(dst, index, srcs, first, count):
        open_dims = [i for i, entry in enumerate(index) if isinstance(entry, slice)]
        where = pl.ds(first, count)

        def at(i):
            full = list(index)
            inner = []
            for position, dim in enumerate(open_dims):
                rank = len(open_dims) - 1 - position
                entry = (i // RING ** rank) % RING
                full[dim] = entry
                inner.append(entry)
            return tuple(full), tuple(inner)

        def body(i, carry):
            full, inner = at(i)
            total = dst[full + (where, slice(None))]
            for src in srcs:
                total += src[inner]
            dst[full + (where, slice(None))] = total
            return carry

        trips = RING ** len(open_dims)
        if trips == 1:
            body(0, 0)
        else:
            lax.fori_loop(0, trips, body, 0)

    order = (2, 1, 3, 0)
    units = [(q, c) for q in range(len(plan[0].chunks)) for c in range(len(plan))]
    keep_copies, part_copies = {}, {}
    slot = 0
    for delta in order:
        for q, c in units:
            index = group(plan[c], 0, delta)
            at = 0
            pieces = []
            for number, (which, first, count) in enumerate(plan[c].chunks[q]):
                span = (pl.ds(first, count), slice(None))
                pieces.append((pltpu.make_async_copy(keep[which].at[index + span], own.at[(c, q) + index + (pl.ds(at, count), slice(None))],
                                                     keep_sem.at[c, q, delta, number]),
                               pltpu.make_async_copy(recv[which].at[index + span], tmp.at[(slot % tmp.shape[0], slice(None), slice(None), pl.ds(at, count), slice(None))],
                                                     part_sem.at[c, q, delta, number])))
                at += count
            keep_copies[q, c, delta] = [p[0] for p in pieces]
            part_copies[q, c, delta] = ([p[1] for p in pieces], slot % tmp.shape[0])
            slot += 1
    for delta in order:
        for q, c in units:
            for copy in keep_copies[q, c, delta]:
                copy.start()
    queue = [(q, c, delta) for delta in order for q, c in units]
    for key in queue[:tmp.shape[0]]:
        for copy in part_copies[key][0]:
            copy.start()
    ahead = list(queue[tmp.shape[0]:])

    def take(q, c, delta):
        copies, where = part_copies[q, c, delta]
        for copy in keep_copies[q, c, delta] + copies:
            copy.wait()
        add_into(own.at[c, q], group(plan[c], 0, delta), [tmp.at[where]], 0, rows)
        if ahead:
            for copy in part_copies[ahead.pop(0)][0]:
                copy.start()

    sends = []

    def send(q, c, phase, step):
        axis = plan[c].axes[phase]
        pair = []
        for way, sign in enumerate((1, -1)):
            target = group(plan[c], phase, 2 if step == 0 else sign)
            span = pl.ds(way * half, half) if step == 0 else slice(None)
            copy = pltpu.make_async_remote_copy(
                own.at[(c, q) + target + (span, slice(None))], got[phase][step].at[c, q, way],
                send_sem.at[c, q, phase, step, way], recv_sem.at[c, q, phase, step, way],
                device_id=neighbor(axis, sign), device_id_type=MESH)
            copy.start()
            pair.append(copy)
        sends.extend(pair)
        return pair

    def land(copies, q, c, phase, step):
        for copy in copies:
            copy.wait_recv()
        bufs = [got[phase][step].at[c, q, way] for way in range(2)]
        if step == 0:
            for way, sign in enumerate((1, -1)):
                add_into(own.at[c, q], group(plan[c], phase, sign), [bufs[way]], way * half, half)
        else:
            add_into(own.at[c, q], group(plan[c], phase, 0), bufs, 0, rows)

    meet([neighbor(axis, sign) for axis in range(3) for sign in (1, -1)])
    flying = {}
    for q, c in units:
        take(q, c, 2)
        flying[q, c] = send(q, c, 0, 0)
    for delta in (1, 3, 0):
        for q, c in units:
            take(q, c, delta)
    for phase in range(3):
        for q, c in units:
            land(flying[q, c], q, c, phase, 0)
            flying[q, c] = send(q, c, phase, 1)
        for q, c in units:
            land(flying[q, c], q, c, phase, 1)
            if phase < 2:
                flying[q, c] = send(q, c, phase + 1, 0)
            else:
                out_ref[c, pl.ds(q * rows, rows), :] = own[(c, q) + coords]
    for copy in sends:
        copy.wait_send()


def rs_call(keep, recv):
    plan = rs_plan()
    colors, chunks = len(plan), len(plan[0].chunks)
    rows = sum(piece[2] for piece in plan[0].chunks[0])
    half = rows // 2
    any_spec = pl.BlockSpec(memory_space=pl.ANY)
    lead = (colors, chunks, 2)
    got = []
    for dims in ((RING, RING), (RING,), ()):
        got += [pltpu.VMEM(lead + dims + (half, LANES), F32), pltpu.VMEM(lead + dims + (rows, LANES), F32)]
    return pl.pallas_call(
        functools.partial(rs_kernel, plan),
        out_shape=jax.ShapeDtypeStruct((colors, chunks * rows, LANES), F32),
        in_specs=[any_spec] * (len(keep) + len(recv)),
        out_specs=pl.BlockSpec(memory_space=pltpu.VMEM),
        scratch_shapes=[pltpu.VMEM((colors, chunks, RING, RING, RING, rows, LANES), F32), pltpu.VMEM((4, RING, RING, rows, LANES), F32)] + got + [
            pltpu.SemaphoreType.DMA((colors, chunks, RING, 2)), pltpu.SemaphoreType.DMA((colors, chunks, RING, 2)),
            pltpu.SemaphoreType.DMA((colors, chunks, 3, 2, 2)), pltpu.SemaphoreType.DMA((colors, chunks, 3, 2, 2))],
        compiler_params=pltpu.CompilerParams(collective_id=2, has_side_effects=True, vmem_limit_bytes=VMEM_MAX),
        name='rs',
    )(*keep, *recv)


def solution(mesh):
    n_dp = mesh.shape['dp']
    dev_count = mesh.shape['cp'] * n_dp
    inv = 1.0 / dev_count
    swap = [(0, 1), (1, 0)]

    def per_device(x_loc, cot_loc, w_q, w_k, w_v, w_o, w_up, w_down):
        d_model, heads, head_dim = w_q.shape
        inner = heads * head_dim
        ff = w_up.shape[1]
        scale = head_dim ** -0.5
        wq, wk, wv, wo = (w.transpose(1, 2, 0).reshape(inner, d_model) for w in (w_q, w_k, w_v, w_o))

        q, k, v, x, g = qkv_call(x_loc, cot_loc, wq, wk, wv)
        o, ot, lse = attn_fwd_call(q, k, v, scale)
        dn_keep, dn_send, up_keep, up_send, o_keep, o_send, gh, go = mlp_call(x, g, o, wo, w_up, w_down, n_dp, inv)
        gq, gk, gv = attn_bwd_call(q, k, v, go, ot, lse, scale)
        qkv_keep, qkv_send = dqkv_call(x, gq, gk, gv, n_dp, inv)
        gx = gx_call(gq, gk, gv, wq, wk, wv, gh)

        def view(arr):
            return arr.reshape(RING, RING, RING, -1, LANES)

        keep = [view(a) for a in (dn_keep, up_keep, o_keep, qkv_keep)]
        recv = [lax.ppermute(view(a), 'cp', swap) for a in (dn_send, up_send, o_send, qkv_send)]
        out = rs_call(keep, recv)

        rows = d_model // dev_count
        g_down = out[0].reshape(-1, d_model // LANES, 8, LANES).transpose(0, 2, 1, 3).reshape(ff // dev_count, d_model)
        g_up = out[1].reshape(ff // LANES, rows, LANES).transpose(1, 0, 2).reshape(rows, ff)
        g_attn = out[2].reshape(4, inner // LANES, rows, LANES).transpose(0, 2, 1, 3).reshape(4, rows, heads, head_dim)
        return gx, g_attn[1], g_attn[2], g_attn[3], g_attn[0], g_up, g_down

    act_spec = P('dp', 'cp', None)
    rep_three = P(None, None, None)
    rep_two = P(None, None)
    grad_three = P(('dp', 'cp'), None, None)
    grad_two = P(('dp', 'cp'), None)
    return jax.shard_map(per_device, mesh=mesh,
                         in_specs=(act_spec, act_spec, rep_three, rep_three, rep_three, rep_three, rep_two, rep_two),
                         out_specs=(act_spec, grad_three, grad_three, grad_three, grad_three, grad_two, grad_two),
                         check_vma=False)
```

time: 931 us -> 301 us (0.32); the launches traced: 921 us -> 301 us
  waiting for transfers between devices: 586 us -> 0.01 us
  Pallas kernels: 0 us -> 292 us
  matrix products: 212 us -> 0 us
  other arithmetic: 60.9 us -> 0 us
  local copies, waits for them, and re-layouts: 46.7 us -> 7.7 us
  between operations: 15.4 us -> 0.72 us
    reduce_scatter x3 -> x0, waiting for transfers between devices: 583 us -> none  [reduce(): lax.psum_scatter(joined.reshape(dev_count * rows, d_model), ('dp', 'cp'),...]
    pallas_call x0 -> x7, Pallas kernels: none -> 292 us  [the longest x1 112 us: rs_call(): pl.pallas_call(functools.partial(rs_kernel, plan), out_shape=jax.ShapeDty...]
    dot_general x41 -> x0, matrix products: 212 us -> none  [the longest x17 123 us: dot(): lax.dot_general(a, b, (dims, ((), ())), preferred_element_type=jnp.float32)]
    concatenate x7 -> x0, other arithmetic: 32.8 us -> none  [the longest x3 31.3 us: reduce(): joined = jnp.concatenate(parts, axis=1)]
    reshape x8 -> x0, local copies, waits for them, and re-layouts: 22 us -> none  [the longest x2 19.2 us: shards(): return (g * inv).reshape(dev_count, -1, d_model)]
    unnamed x185 -> x1, local copies, waits for them, and re-layouts: 13.9 us -> 3.08 us
    reduce_sum x4 -> x0, other arithmetic: 10.1 us -> none  [per_device(): l = e.sum(axis=-1)]
  transfers between devices with their start and end apart: 6 -> 4, of which waited for: 4 -> 0; matrix products, arithmetic and copies ran while one was open for 16% -> 0% of each run, Pallas kernels for 0% -> 21%
where the time goes in v2:
time: 301 us
  Pallas kernels  292 us (97%)
  local copies, waits for them, and re-layouts  7.7 us (3%)
    pallas_call x1, Pallas kernels, rs_call(): pl.pallas_call(functools.partial(rs_kernel, plan), out_shape=jax.ShapeDty...  112 us
    pallas_call x1, Pallas kernels, mlp_call(): pl.pallas_call(functools.partial(mlp_kernel, inv, n_dp), grid=(steps,), o...  68.8 us
    pallas_call x1, Pallas kernels, attn_bwd_call(): pl.pallas_call(functools.partial(attn_bwd_kernel, scale), grid=(pairs,),...  36 us
    pallas_call x1, Pallas kernels, attn_fwd_call(): pl.pallas_call(functools.partial(attn_fwd_kernel, scale), grid=(pairs,),...  32.9 us
    pallas_call x1, Pallas kernels, qkv_call(): pl.pallas_call(qkv_kernel, out_shape=[act] * 5, in_specs=[any_spec] * 2 +...  14.9 us
    pallas_call x1, Pallas kernels, gx_call(): pl.pallas_call(gx_kernel, out_shape=jax.ShapeDtypeStruct((2, tok // 2, d_...  14.1 us
    pallas_call x1, Pallas kernels, dqkv_call(): pl.pallas_call(functools.partial(dqkv_kernel, inv, n_dp), grid=(inner //...  12.5 us
  transfers between devices with their start and end apart: 4, of which 0 were waited for; matrix products, arithmetic and copies ran while one was open for 0% of the time, Pallas kernels for 21%

profile of v2, /device:TPU:0, one launch (start us, length us, event | category | flops | bytes accessed | tf_op | source)
XLA Modules:
  0.0 301.2 jit_solution(10039282019473831693)
XLA Ops:
  0.6 14.9 %qkv.1 = (bf16[1024,1024]{1,0:T(8,128)(2,1)}, bf16[1024,1024]{1,0:T(8,128)(2,1)}, bf16[1024,1024]{1,0:T(8,128)(2,1)}, bf16[1024,1024]{1,0:T(8,128)(2,1)}, bf16[1024,1024]{1,0:T(8,128)(2,1)}) custom-call(bf16[2,512,1024]{2,1,0:T(8,128)(2,1)} %x_hbm.1, bf16[2,512,1024]{2,1,0:T(8,128)(2,1)} %g_hbm.1, bf16[1024,1024]{1,0:T(8,128)(2,1)} %bitcast.42, ...), custom_call_target="tpu_custom_call" | custom-call | tf_op jit(solution)/shard_map/qkv/pallas_call | solution.py:90
  15.6 32.9 %attn_fwd.1 = (bf16[1024,1024]{1,0:T(8,128)(2,1)}, f32[1024,1024]{1,0:T(8,128)}, f32[8,2,1024]{2,1,0:T(2,128)}) custom-call(bf16[1024,1024]{1,0:T(8,128)(2,1)} %get-tuple-element.28.q_ref, bf16[1024,1024]{1,0:T(8,128)(2,1)} %get-tuple-element.29.k_ref, bf16[1024,1024]{1,0:T(8,128)(2,1)} %get-tuple-element.30.v_ref), custom_call_target="tpu_custom_call" | custom-call | flops 4294967296 | bytes 12582912 | tf_op jit(solution)/shard_map/attn_fwd/pallas_call | solution.py:144
  48.4 68.8 %mlp.1 = (f32[64,4,8,8,128]{4,3,2,1,0:T(8,128)}, f32[64,4,8,8,128]{4,3,2,1,0:T(8,128)}, f32[64,32,8,128]{3,2,1,0:T(8,128)}, f32[64,32,8,128]{3,2,1,0:T(8,128)}, ...) custom-call(bf16[1024,1024]{1,0:T(8,128)(2,1)} %get-tuple-element.31.x, ...), custom_call_target="tpu_custom_call" | custom-call | flops 42949672960 | bytes 33554432 | tf_op jit(solution)/shard_map/mlp/pallas_call | solution.py:279
  117.2 0.1 collective-permute-start
  117.3 0.5 collective-permute-start.1
  117.8 36.0 %attn_bwd.1 = (bf16[1024,1024]{1,0:T(8,128)(2,1)}, bf16[1024,1024]{1,0:T(8,128)(2,1)}, bf16[1024,1024]{1,0:T(8,128)(2,1)}) custom-call(bf16[1024,1024]{1,0:T(8,128)(2,1)} %get-tuple-element.28.q_ref, bf16[1024,1024]{1,0:T(8,128)(2,1)} %get-tuple-element.29.k_ref, bf16[1024,1024]{1,0:T(8,128)(2,1)} %get-tuple-element.30.v_ref, ...), custom_call_target="tpu_custom_call" | custom-call | flops 10737418240 | bytes 18874368 | tf_op jit(solution)/shard_map/attn_bwd/pallas_call | solution.py:199
  153.8 12.5 %dqkv.1 = (f32[64,3,8,8,128]{4,3,2,1,0:T(8,128)}, f32[64,3,8,8,128]{4,3,2,1,0:T(8,128)}) custom-call(bf16[1024,1024]{1,0:T(8,128)(2,1)} %get-tuple-element.31.x_ref, bf16[1024,1024]{1,0:T(8,128)(2,1)} %get-tuple-element.37.gq_ref, bf16[1024,1024]{1,0:T(8,128)(2,1)} %get-tuple-element.38.gk_ref, bf16[1024,1024]{1,0:T(8,128)(2,1)} %get-tuple-element.39.gv_ref), custom_call_target="tpu_custom_call" | custom-call | flops 6442450944 | bytes 12582912 | tf_op jit(solution)/shard_map/dqkv/pallas_call | solution.py:311
  166.3 0.2 collective-permute-start.3
  166.5 0.3 collective-permute-start.2
  166.8 14.1 %gx.1 = bf16[2,512,1024]{2,1,0:T(8,128)(2,1)} custom-call(bf16[1024,1024]{1,0:T(8,128)(2,1)} %get-tuple-element.37.gq_ref, bf16[1024,1024]{1,0:T(8,128)(2,1)} %get-tuple-element.38.gk_ref, bf16[1024,1024]{1,0:T(8,128)(2,1)} %get-tuple-element.39.gv_ref, bf16[1024,1024]{1,0:T(8,128)(2,1)} %bitcast.43, bf16[1024,1024]{1,0:T(8,128)(2,1)} %bitcast.45, ...), custom_call_target="tpu_custom_call" | custom-call | tf_op jit(solution)/shard_map/gx/pallas_call | solution.py:352
  180.9 0.0 collective-permute-done.2.refs_6_
  180.9 0.0 collective-permute-done.3.refs_7_
  181.0 0.0 collective-permute-done.refs_4_
  181.0 0.0 collective-permute-done.1.refs_5_
  181.0 112.5 %rs.1 = f32[3,256,128]{2,1,0:T(8,128)} custom-call(f32[4,4,4,256,128]{4,3,2,1,0:T(8,128)} %bitcast.48, f32[4,4,4,256,128]{4,3,2,1,0:T(8,128)} %bitcast.49, f32[4,4,4,64,128]{4,3,2,1,0:T(8,128)} %bitcast.51, f32[4,4,4,192,128]{4,3,2,1,0:T(8,128)} %bitcast.50, f32[4,4,4,256,128]{4,3,2,1,0:T(8,128)} %collective-permute-done.refs_4_, ...), custom_call_target="tpu_custom_call" | custom-call | tf_op jit(solution)/shard_map/rs/pallas_call | solution.py:524
  293.4 1.8 fusion
  295.2 0.7 squeeze.15
  295.9 0.7 squeeze.14
  296.7 0.7 squeeze.13
  297.4 0.7 squeeze.12
  298.1 3.1 %copy.20 = bf16[2,512,1024]{2,1,0:T(8,128)(2,1)} copy(bf16[2,512,1024]{2,1,0:T(8,128)(2,1)} %gx.1) | data formatting | bytes 4194304
  (5 shorter events, 0.0 us)
Async XLA Ops:
  117.2 63.7 %collective-permute-start = (f32[4,4,4,256,128]{4,3,2,1,0:T(8,128)}, f32[4,4,4,256,128]{4,3,2,1,0:T(8,128)}, u32[]{:S(2)}, u32[]{:S(2)}) collective-permute-start(f32[4,4,4,256,128]{4,3,2,1,0:T(8,128)} %bitcast.55), channel_id=1, source_target_pairs={{0,1},{1,0},{2,3},{3,2},{4,5},{5,4},{6,7},{7,6},{8,9},{9,8},{10,11... | collective-permute-start | bytes 25165832 | tf_op jit(solution)/shard_map/ppermute | solution.py:561
  117.3 63.6 %collective-permute-start.1 = (f32[4,4,4,256,128]{4,3,2,1,0:T(8,128)}, f32[4,4,4,256,128]{4,3,2,1,0:T(8,128)}, u32[]{:S(2)}, u32[]{:S(2)}) collective-permute-start(f32[4,4,4,256,128]{4,3,2,1,0:T(8,128)} %bitcast.54), channel_id=1, source_target_pairs={{0,1},{1,0},{2,3},{3,2},{4,5},{5,4},{6,7},{7,6},{8,9},{9,8},{10,11... | collective-permute-start | bytes 25165832 | tf_op jit(solution)/shard_map/ppermute | solution.py:561
  166.3 14.7 %collective-permute-start.3 = (f32[4,4,4,192,128]{4,3,2,1,0:T(8,128)}, f32[4,4,4,192,128]{4,3,2,1,0:T(8,128)}, u32[]{:S(2)}, u32[]{:S(2)}) collective-permute-start(f32[4,4,4,192,128]{4,3,2,1,0:T(8,128)} %bitcast.56), channel_id=1, source_target_pairs={{0,1},{1,0},{2,3},{3,2},{4,5},{5,4},{6,7},{7,6},{8,9},{9,8},{10,11... | collective-permute-start | bytes 18874376 | tf_op jit(solution)/shard_map/ppermute | solution.py:561
  166.5 14.4 %collective-permute-start.2 = (f32[4,4,4,64,128]{4,3,2,1,0:T(8,128)}, f32[4,4,4,64,128]{4,3,2,1,0:T(8,128)}, u32[]{:S(2)}, u32[]{:S(2)}) collective-permute-start(f32[4,4,4,64,128]{4,3,2,1,0:T(8,128)} %bitcast.58), channel_id=1, source_target_pairs={{0,1},{1,0},{2,3},{3,2},{4,5},{5,4},{6,7},{7,6},{8,9},{9,8},{10,11... | collective-permute-start | bytes 6291464 | tf_op jit(solution)/shard_map/ppermute | solution.py:561
